TPU v7x, 256 devices: a whole 4x4x8 slice. The times are simulated.
256 devices in a mesh: win: 128 (over y, x, z), head: 2 (over core).
Axes of the slice: x: 4, y: 4, z: 8, core: 2. Of those that a mesh axis runs over, the one named last changes fastest.
Arguments:
- coords: float32 [3, 4096, 128], P(None, 'win', 'head'), may hold values from -8 to 16
- noise: float32 [3, 4096, 128], P(None, 'win', 'head'), may hold values from -6 to 6
- sigma: float32 [1], replicated, may hold values from 0.25 to 1
- atom_single: bfloat16 [4096, 128, 128], P('win', 'head'), may hold values from -6 to 6
- token_single: bfloat16 [65536, 384], P('win'), may hold values from -6 to 6
- atom_token: int32 [4096, 128], P('win', 'head'), may hold values from 0 to 15, never falling along the last dimension, each value on 1 to 64 neighbouring positions
- window_count: int32 [128], replicated, may hold values from 1 to 31, as said below
- pair_bias: bfloat16 [4, 4096, 128, 128], P('head', 'win'), may hold values from -6 to 260
- token_weight: bfloat16 [384, 128], replicated, may hold values from -0.3125 to 0.3125
- cond_gain: float32 [128], replicated, may hold values from 0.25 to 1.75
- position_weight: float32 [3, 128], replicated, may hold values from -3.5 to 3.5
- ada_weight: bfloat16 [3, 6, 128, 128], replicated, may hold values from -0.5 to 0.5
- ada_bias: float32 [3, 6, 128], replicated, may hold values from -4 to 4
- attn_weight: bfloat16 [3, 4, 128, 128], P(None, None, None, 'head'), may hold values from -0.5 to 0.5
- out_weight: bfloat16 [3, 128, 128], P(None, 'head'), may hold values from -0.5 to 0.5
- gateup_weight: bfloat16 [3, 2, 128, 256], replicated, may hold values from -0.5 to 0.5
- down_weight: bfloat16 [3, 256, 128], replicated, may hold values from -0.375 to 0.375
- final_weight: bfloat16 [3, 128], replicated, may hold values from -0.5 to 0.5
Outputs:
- denoised: float32 [3, 4096, 128], P(None, 'win', 'head')
Inputs may be any that keep to these rules, and one draw needn't show every extreme that they name: window_count[d] + window_count[d + 64] <= 32 for every d < 64, with equality for some d.
All inputs are finite; a program needn't handle non-finite values.
Results may differ from a plain program's by a relative error of at most 0.005.
Values may be sent and summed in bfloat16 or wider, within the bound.
A program may use at most 128 MiB of HBM per device.

v0:
```python
import jax
import jax.numpy as jnp
from jax import lax
from jax.sharding import Mesh
from jax.sharding import PartitionSpec as P

HEAD_DIM = 32
QW = 128
TOKW = 16
BLOCKS = 3
WIN = ("win_0", "win_1", "win_2")
WIN_HEAD = ("win_0", "win_1", "win_2", "head")
EPSILON = 1e-05


def rows_first(arrays, axis, dims):
    turned = [jnp.moveaxis(a, dim, 0) for a, dim in zip(arrays, dims)]
    widths = [t[0].size for t in turned]
    both = jnp.concatenate([t.reshape(-1, w) for t, w in zip(turned, widths)], axis=1)
    filled = lax.all_gather(both, axis, axis=0, tiled=True)
    parts = jnp.split(filled, [sum(widths[:k]) for k in range(1, len(widths))], axis=1)
    return tuple(
        (
            jnp.moveaxis(b.reshape(-1, *t.shape[1:]), 0, dim)
            for b, t, dim in zip(parts, turned, dims)
        )
    )


def in_one_piece(arrays, axis, split_dim, concat_dim, along):
    ends, at = ([], 0)
    for a in arrays[:-1]:
        at += a.shape[along]
        ends.append(at)
    both = jnp.concatenate(arrays, axis=along)
    return tuple(
        jnp.split(
            lax.all_to_all(both, axis, split_axis=split_dim, concat_axis=concat_dim, tiled=True),
            ends,
            axis=along,
        )
    )


def by_axis(array, axes):
    for axis in axes:
        array = lax.psum(array, axis)
    return array


def layer_norm(values):
    average = jnp.mean(values, axis=-1, keepdims=True)
    centred = values - average
    variance = jnp.mean(centred * centred, axis=-1, keepdims=True)
    return centred * lax.rsqrt(variance + EPSILON)


def lookup_tokens(tokens_here, local_token):
    token_grid = tokens_here.reshape(local_token.shape[0], TOKW, -1)
    one_hot = (local_token[:, :, None] == jnp.arange(TOKW, dtype=jnp.int32)).astype(jnp.bfloat16)
    return jnp.einsum(
        "wqt,wtc->wqc", one_hot, token_grid, preferred_element_type=jnp.float32
    ).astype(jnp.bfloat16)


def project_rows(weight_set, portion):
    return jnp.einsum(
        "wqc,jcd->jwqd", portion, weight_set, preferred_element_type=jnp.float32
    ).astype(jnp.bfloat16)


def window_net(single, looked, scaled, pair_terms, weights_all, project_fn, output_fn):
    cond_gain, position_weight, ada_weight, ada_bias, gateup_weight, down_weight, final_weight = (
        weights_all
    )
    condition = single.astype(jnp.float32) + looked.astype(jnp.float32)
    cond_norm = (layer_norm(condition) * cond_gain).astype(jnp.bfloat16)
    stream = condition + jnp.einsum(
        "kwq,kc->wqc", scaled, position_weight, precision=lax.Precision.HIGHEST
    )
    window_total = single.shape[0]
    for block_index in range(BLOCKS):
        ada_terms = (
            jnp.einsum(
                "wqc,jcd->jwqd",
                cond_norm,
                ada_weight[block_index],
                preferred_element_type=jnp.float32,
            )
            + ada_bias[block_index][:, None, None, :]
        )
        normed = (layer_norm(stream) * jax.nn.sigmoid(ada_terms[0]) + ada_terms[1]).astype(
            jnp.bfloat16
        )
        projected = project_fn(block_index, normed)
        row_count = projected.shape[2]
        query_rows = projected[0].reshape(window_total, row_count, -1, HEAD_DIM)
        key_rows = projected[1].reshape(window_total, row_count, -1, HEAD_DIM)
        value_rows = projected[2].reshape(window_total, row_count, -1, HEAD_DIM)
        gate_logits = (
            projected[3].reshape(window_total, row_count, -1, HEAD_DIM).astype(jnp.float32)
        )
        scores = jnp.einsum(
            "wqhd,wkhd->hwqk", query_rows, key_rows, preferred_element_type=jnp.float32
        )
        scores = scores * HEAD_DIM ** (-0.5) + pair_terms.astype(jnp.float32)
        row_max = jnp.max(scores, axis=-1, keepdims=True)
        exponent = jnp.exp(scores - row_max)
        weights = (exponent / jnp.sum(exponent, axis=-1, keepdims=True)).astype(jnp.bfloat16)
        attended = jnp.einsum(
            "hwqk,wkhd->wqhd", weights, value_rows, preferred_element_type=jnp.float32
        )
        attended = (
            (attended * jax.nn.sigmoid(gate_logits))
            .astype(jnp.bfloat16)
            .reshape(window_total, row_count, -1)
        )
        update = output_fn(block_index, attended)
        stream = stream + jax.nn.sigmoid(ada_terms[2]) * update
        normed_two = (layer_norm(stream) * jax.nn.sigmoid(ada_terms[3]) + ada_terms[4]).astype(
            jnp.bfloat16
        )
        gate_part = jnp.einsum(
            "wqc,ch->wqh",
            normed_two,
            gateup_weight[block_index, 0],
            preferred_element_type=jnp.float32,
        )
        up_part = jnp.einsum(
            "wqc,ch->wqh",
            normed_two,
            gateup_weight[block_index, 1],
            preferred_element_type=jnp.float32,
        )
        hidden = (jax.nn.silu(gate_part) * up_part).astype(jnp.bfloat16)
        down_part = jnp.einsum(
            "wqh,hc->wqc", hidden, down_weight[block_index], preferred_element_type=jnp.float32
        )
        stream = stream + jax.nn.sigmoid(ada_terms[5]) * down_part
    final_norm = layer_norm(stream).astype(jnp.bfloat16)
    return jnp.einsum("wqc,kc->kwq", final_norm, final_weight, preferred_element_type=jnp.float32)


def run_net(single, looked, scaled, pair_terms, weights_all, attn_weight, out_weight):
    attn_full, out_full = rows_first((attn_weight, out_weight), "head", (3, 1))
    single_own, looked_own = in_one_piece((single, looked), "head", 0, 1, 2)
    terms_own = lax.all_to_all(pair_terms, "head", split_axis=1, concat_axis=0, tiled=True)
    scaled_own = lax.all_to_all(scaled, "head", split_axis=1, concat_axis=2, tiled=True)

    def project_local(block_index, normed):
        return project_rows(attn_full[block_index], normed)

    def output_local(block_index, attended):
        return jnp.einsum(
            "wqd,dc->wqc", attended, out_full[block_index], preferred_element_type=jnp.float32
        )

    update_own = window_net(
        single_own, looked_own, scaled_own, terms_own, weights_all, project_local, output_local
    )
    return lax.all_to_all(update_own, "head", split_axis=2, concat_axis=1, tiled=True)


def local(
    coords,
    noise,
    sigma,
    atom_single,
    token_single,
    atom_token,
    window_count,
    pair_bias,
    token_weight,
    cond_gain,
    position_weight,
    ada_weight,
    ada_bias,
    attn_weight,
    out_weight,
    gateup_weight,
    down_weight,
    final_weight,
):
    sigma_value = sigma[0]
    noisy_pos = coords + sigma_value * noise
    slot_total = atom_single.shape[0]
    device_id = lax.axis_index(WIN)
    own_count = window_count[device_id]
    slot_ids = jnp.arange(slot_total, dtype=jnp.int32)
    live_mask = (slot_ids < own_count).astype(jnp.float32)
    partial_pos = jnp.sum(noisy_pos * live_mask[None, :, None], axis=(1, 2))
    totals = by_axis(partial_pos, WIN_HEAD)
    centre = totals / (QW * jnp.sum(window_count).astype(jnp.float32))
    shifted = noisy_pos - centre[:, None, None]
    inverse = 1.0 / (1.0 + sigma_value * sigma_value)
    scaled = shifted * jnp.sqrt(inverse)
    token_proj = jnp.dot(token_single, token_weight, preferred_element_type=jnp.float32).astype(
        jnp.bfloat16
    )
    looked = lookup_tokens(token_proj, atom_token)
    weights_all = (
        cond_gain,
        position_weight,
        ada_weight,
        ada_bias,
        gateup_weight,
        down_weight,
        final_weight,
    )
    update_pos = run_net(
        atom_single, looked, scaled, pair_bias, weights_all, attn_weight, out_weight
    )
    denoised = shifted * inverse + sigma_value * jnp.sqrt(inverse) * update_pos
    return denoised * live_mask[None, :, None]


def solution(mesh):
    torus = Mesh(
        mesh.devices.reshape(4, 4, 8, mesh.shape["head"]), ("win_0", "win_1", "win_2", "head")
    )
    in_specs = (
        P(None, WIN, "head"),
        P(None, WIN, "head"),
        P(),
        P(WIN, "head", None),
        P(WIN, None),
        P(WIN, "head"),
        P(),
        P("head", WIN, None, None),
        P(),
        P(),
        P(),
        P(),
        P(),
        P(None, None, None, "head"),
        P(None, "head", None),
        P(),
        P(),
        P(),
    )
    out_specs = P(None, WIN, "head")
    return jax.shard_map(local, mesh=torus, in_specs=in_specs, out_specs=out_specs, check_vma=False)
```

profile of v0, /device:TPU:1, one launch (start us, length us, event | category | flops | bytes accessed | tf_op | source)
XLA Modules:
  0.0 160.6 jit_solution(1262722235757631288)
XLA Ops:
  3.7 9.5 %psum.28 = f32[3]{0:T(128)S(1)} all-reduce(f32[3]{0:T(128)S(1)} %get-tuple-element.5), channel_id=1, replica_groups=mesh['win_0'=4,'win_1'=4,'win_2'=8,'head'=2] {'win_0'}, use_global_device_ids=true, to_apply=%region_1.0 | all-reduce | flops 3 | bytes 24 | tf_op jit(solution)/shard_map/psum | solution.py:47
  14.5 8.7 %psum.29 = f32[3]{0:T(128)S(1)} all-reduce(f32[3]{0:T(128)S(1)} %psum.28), channel_id=1, replica_groups=mesh['win_0'=4,'win_1'=4,'win_2'=8,'head'=2] {'win_1'}, use_global_device_ids=true, to_apply=%region_2.0 | all-reduce | flops 3 | bytes 24 | tf_op jit(solution)/shard_map/psum | solution.py:47
  23.3 16.2 %psum.30 = f32[3]{0:T(128)S(1)} all-reduce(f32[3]{0:T(128)S(1)} %psum.29), channel_id=1, replica_groups=mesh['win_0'=4,'win_1'=4,'win_2'=8,'head'=2] {'win_2'}, use_global_device_ids=true, to_apply=%region_3.0 | all-reduce | flops 3 | bytes 24 | tf_op jit(solution)/shard_map/psum | solution.py:47
  39.6 10.3 %psum.31 = f32[3]{0:T(128)S(1)} all-reduce(f32[3]{0:T(128)S(1)} %psum.30), channel_id=1, replica_groups=mesh['win_0'=4,'win_1'=4,'win_2'=8,'head'=2] {'head'}, use_global_device_ids=true, to_apply=%region_4.0 | all-reduce | flops 3 | bytes 24 | tf_op jit(solution)/shard_map/psum | solution.py:47
  51.4 3.6 %all-to-all-start.1 = ((f32[2,1,3072]{2,1,0:T(1,128)}), f32[2,1,3072]{2,1,0:T(1,128)S(1)}, u32[]{:S(2)}, u32[]{:S(2)}) async-start(f32[2,1,3072]{2,1,0:T(1,128)} %reshape.274), calls=%async_computation.1 | async-start | bytes 49152 | tf_op jit(solution)/shard_map/all_to_all | solution.py:148
  57.4 2.2 %pad_maximum_fusion = bf16[32,64,256]{2,1,0:T(8,128)(2,1)} fusion(bf16[32,64,128]{2,1,0:T(8,128)(2,1)S(1)} %convolution_convert_fusion, bf16[32,64,128]{2,1,0:T(8,128)(2,1)} %param.21), kind=kLoop, calls=%fused_computation.139 | loop fusion | flops 2097152 | bytes 2097152 | tf_op jit(solution)/shard_map/concatenate | solution.py:35
  60.2 3.6 %all-to-all-start = ((bf16[32,64,256]{2,1,0:T(8,128)(2,1)}), bf16[32,64,256]{2,1,0:T(8,128)(2,1)S(1)}, u32[]{:S(2)}, u32[]{:S(2)}) async-start(bf16[32,64,256]{2,1,0:T(8,128)(2,1)} %pad_maximum_fusion), calls=%async_computation | async-start | bytes 2097152 | tf_op jit(solution)/shard_map/all_to_all | solution.py:38
  67.4 3.8 %all-to-all-start.2 = ((bf16[2,32,128,128]{3,2,0,1:T(8,128)(2,1)}), bf16[2,32,128,128]{3,2,0,1:T(8,128)(2,1)S(1)}, u32[]{:S(2)}, u32[]{:S(2)}) async-start(bf16[2,32,128,128]{3,2,0,1:T(8,128)(2,1)} %copy.260), calls=%async_computation.2 | async-start | bytes 4194304 | tf_op jit(solution)/shard_map/all_to_all | solution.py:147
  80.3 2.3 %all_gather.3 = bf16[128,1920]{1,0:T(8,128)(2,1)S(1)} all-gather(bf16[64,1920]{1,0:T(8,128)(2,1)S(1)} %pad_maximum_fusion.1), channel_id=1, replica_groups=mesh['win_0'=4,'win_1'=4,'win_2'=8,'head'=2] {'head'}, dimensions={0}, use_global_device_ids=true | all-gather | bytes 737280 | tf_op jit(solution)/shard_map/all_gather | solution.py:20
  88.4 2.0 %add_bitcast_fusion.2 = f32[6,16,128,128]{2,3,1,0:T(8,128)S(1)} fusion(f32[6,128]{1,0:T(8,128)S(1)} %get-tuple-element.19, bf16[16,128,128,1]{1,2,0,3:T(8,128)(2,1)S(1)} %fusion.118, bf16[3,6,128,128]{3,2,1,0:T(8,128)(2,1)} %param.29), kind=kOutput, calls=%fused_computation.5 | convolution fusion | flops 404226048 | bytes 7015424 | tf_op jit(solution)/shard_map/wqc,jcd->jwqd/dot_general | solution.py:84
  94.3 3.1 %copy.261 = f32[2,2,16,128,128]{3,4,2,0,1:T(8,128)} copy(bf16[2,2,16,128,128]{4,3,0,2,1:T(8,128)(2,1)S(1)} %bitcast.376) | data formatting | bytes 6291456 | tf_op jit(solution)/shard_map/convert_element_type | solution.py:106
  97.4 3.0 %bitcast_add_fusion.2 = f32[4,16,128,128]{2,3,1,0:T(8,128)S(1)} fusion(f32[2,2,16,128,128]{3,4,2,0,1:T(8,128)} %copy.261, bf16[16,128,4,32]{1,3,2,0:T(8,128)(2,1)S(1)} %bitcast.380, bf16[16,128,4,32]{1,3,2,0:T(8,128)(2,1)S(1)} %bitcast.379), kind=kOutput, calls=%fused_computation.8 | convolution fusion | flops 69206016 | bytes 9437184 | tf_op jit(solution)/shard_map/wqhd,wkhd->hwqk/dot_general | solution.py:103
  100.4 2.8 %fusion.188 = (f32[4,16,128]{2,1,0:T(8,128)S(1)}, f32[4,16,128,128]{2,3,1,0:T(8,128)}) fusion(f32[4,16,128,128]{2,3,1,0:T(8,128)S(1)} %bitcast_add_fusion.2), kind=kOutput, calls=%fused_computation.255 | output fusion | flops 2097279 | bytes 8421376 | tf_op jit(solution)/shard_map/sub | solution.py:108
  103.4 3.2 %fusion.39 = bf16[16,128,4,32]{1,3,2,0:T(8,128)(2,1)S(1)} fusion(f32[16,128,4,32]{1,3,2,0:T(8,128)S(1)} %bitcast.386, bf16[16,128,4,32]{1,3,2,0:T(8,128)(2,1)} %bitcast.392, f32[4,16,128,128]{2,3,1,0:T(8,128)} %get-tuple-element.24, f32[4,16,128]{2,1,0:T(8,128)S(1)} %get-tuple-element.23), kind=kOutput, calls=%fused_computation.49 | convolution fusion | flops 69730304 | bytes 6324224 | tf_op jit(solution)/shard_map/hwqk,wkhd->wqhd/dot_general | solution.py:110
  108.3 4.6 %add_bitcast_fusion.1 = f32[6,16,128,128]{2,3,1,0:T(8,128)} fusion(f32[6,128]{1,0:T(8,128)S(1)} %get-tuple-element.20, bf16[16,128,128,1]{1,2,0,3:T(8,128)(2,1)S(1)} %copy-done.7, bf16[3,6,128,128]{3,2,1,0:T(8,128)(2,1)} %param.29), kind=kOutput, calls=%fused_computation.4 | convolution fusion | flops 404226048 | bytes 7015424 | tf_op jit(solution)/shard_map/wqc,jcd->jwqd/dot_general | solution.py:84
  114.2 3.8 %fusion.190 = (f32[16,128]{1,0:T(8,128)S(1)}, f32[16,128,128]{1,2,0:T(8,128)}) fusion(f32[16,128,128]{1,2,0:T(8,128)} %copy-done.8, bf16[3,256,128]{2,1,0:T(8,128)(2,1)} %param.34, f32[16,128,256]{2,1,0:T(8,128)S(1)} %fusion.157, bf16[16,128,128]{1,2,0:T(8,128)(2,1)S(1)} %fusion.93, bf16[3,2,128,256]{3,2,1,0:T(8,128)(2,1)} %param.33, ...), kind=kOutput, calls=%fused_computation.257 | convolution fusion | flops 273152000 | bytes 5906432 | tf_op jit(solution)/shard_map/wqh,hc->wqc/dot_general | solution.py:136
  119.4 2.8 %convert_bitcast_fusion.1 = bf16[4,16,128,128]{2,3,1,0:T(8,128)(2,1)S(1)} fusion(f32[6,16,128,128]{2,3,1,0:T(8,128)} %add_bitcast_fusion.1, f32[16,128,128]{1,2,0:T(8,128)} %get-tuple-element.28, f32[16,128]{1,0:T(8,128)S(1)} %add_rsqrt_fusion.4, f32[16,128]{1,0:T(8,128)S(1)} %broadcast_multiply_fusion.5, bf16[3,4,128,128]{2,3,1,0:T(8,128)(2,1)S(1)} %bitcast.396), kind=kOutput, calls=%fused_computation.24 | convolution fusion | flops 271581184 | bytes 5390336 | tf_op jit(solution)/shard_map/wqc,jcd->jwqd/dot_general | solution.py:67
  123.4 4.1 %fusion.193 = (f32[4,16,128]{2,1,0:T(8,128)S(1)}, f32[4,16,128,128]{2,3,1,0:T(8,128)S(1)}) fusion(f32[4,16,128,128]{2,3,1,0:T(8,128)S(1)} %bitcast_add_fusion.1), kind=kOutput, calls=%fused_computation.258 | output fusion | flops 2097279 | bytes 8421376 | tf_op jit(solution)/shard_map/sub | solution.py:108
  132.9 4.0 %fusion.195 = (f32[16,128]{1,0:T(8,128)S(1)}, f32[16,128,128]{1,2,0:T(8,128)}) fusion(f32[16,128,128]{1,2,0:T(8,128)S(1)} %get-tuple-element.32, bf16[3,256,128]{2,1,0:T(8,128)(2,1)} %param.34, f32[16,128,256]{2,1,0:T(8,128)} %fusion.153, bf16[16,128,128]{1,2,0:T(8,128)(2,1)S(1)} %fusion.71, bf16[3,2,128,256]{3,2,1,0:T(8,128)(2,1)S(1)} %copy-done.24, ...), kind=kOutput, calls=%fused_computation.260 | convolution fusion | flops 273152000 | bytes 5906432 | tf_op jit(solution)/shard_map/wqh,hc->wqc/dot_general | solution.py:136
  136.9 2.0 %add_bitcast_fusion = f32[6,16,128,128]{2,3,1,0:T(8,128)S(1)} fusion(f32[6,128]{1,0:T(8,128)S(1)} %get-tuple-element.18, bf16[16,128,128,1]{1,2,0,3:T(8,128)(2,1)S(1)} %copy-done.7, bf16[3,6,128,128]{3,2,1,0:T(8,128)(2,1)} %param.29), kind=kOutput, calls=%fused_computation.3 | convolution fusion | flops 404226048 | bytes 7015424 | tf_op jit(solution)/shard_map/wqc,jcd->jwqd/dot_general | solution.py:84
  140.3 3.1 %copy-done.3 = f32[2,2,16,128,128]{3,4,2,0,1:T(8,128)S(1)} copy-done((f32[2,2,16,128,128]{3,4,2,0,1:T(8,128)S(1)}, f32[2,2,16,128,128]{3,4,2,0,1:T(8,128)}, u32[]{:S(2)}) %copy-start.3) | copy-done | bytes 4194328
  144.2 3.9 %fusion.198 = (f32[4,16,128]{2,1,0:T(8,128)S(1)}, f32[4,16,128,128]{2,3,1,0:T(8,128)S(1)}) fusion(f32[4,16,128,128]{2,3,1,0:T(8,128)S(1)} %bitcast_add_fusion), kind=kOutput, calls=%fused_computation.261 | output fusion | flops 2097279 | bytes 8421376 | tf_op jit(solution)/shard_map/sub | solution.py:108
  151.5 3.0 %fusion.200 = (f32[16,128]{1,0:T(8,128)S(1)}, f32[16,128,128]{1,2,0:T(8,128)S(1)}) fusion(f32[16,128,128]{1,2,0:T(8,128)S(1)} %get-tuple-element.38, bf16[3,256,128]{2,1,0:T(8,128)(2,1)} %param.34, f32[16,128,256]{2,1,0:T(8,128)} %fusion.149, bf16[16,128,128]{1,2,0:T(8,128)(2,1)S(1)} %fusion.49, bf16[3,2,128,256]{3,2,1,0:T(8,128)(2,1)S(1)} %copy-done.24, ...), kind=kOutput, calls=%fused_computation.263 | convolution fusion | flops 273152000 | bytes 5906432 | tf_op jit(solution)/shard_map/wqh,hc->wqc/dot_general | solution.py:136
  155.3 3.5 %all_to_all.54 = f32[2,1,3072]{2,1,0:T(1,128)S(1)} all-to-all(f32[2,1,3072]{2,1,0:T(1,128)S(1)} %reshape.276), channel_id=1, replica_groups=mesh['win_0'=4,'win_1'=4,'win_2'=8,'head'=2] {'head'}, dimensions={0} | all-to-all | bytes 49152 | tf_op jit(solution)/shard_map/all_to_all | solution.py:161
  (171 shorter events, 49.3 us)
Async XLA Ops:
  0.0 55.0 %copy-start = (bf16[512,384]{1,0:T(8,128)(2,1)S(1)}, bf16[512,384]{1,0:T(8,128)(2,1)}, u32[]{:S(2)}) copy-start(bf16[512,384]{1,0:T(8,128)(2,1)} %param.22) | copy-start | bytes 1179652
  0.0 65.9 %copy-start.12 = (bf16[2,32,128,128]{3,2,1,0:T(8,128)(2,1)S(1)}, bf16[2,32,128,128]{3,2,1,0:T(8,128)(2,1)}, u32[]{:S(2)}) copy-start(bf16[2,32,128,128]{3,2,1,0:T(8,128)(2,1)} %param.25) | copy-start | bytes 6291460
  3.7 55.9 %copy-start.17 = (f32[3,32,64]{2,1,0:T(8,128)}, f32[3,32,64]{2,1,0:T(8,128)S(1)}, u32[]{:S(2)}) copy-start(f32[3,32,64]{2,1,0:T(8,128)S(1)} %get-tuple-element.6) | copy-start | bytes 73732
  50.6 16.8 %copy-start.32 = (f32[3]{0:T(128)}, f32[3]{0:T(128)S(1)}, u32[]{:S(2)}) copy-start(f32[3]{0:T(128)S(1)} %broadcast_divide_fusion) | copy-start | bytes 40
  51.4 8.1 %all-to-all-start.1 = ((f32[2,1,3072]{2,1,0:T(1,128)}), f32[2,1,3072]{2,1,0:T(1,128)S(1)}, u32[]{:S(2)}, u32[]{:S(2)}) async-start(f32[2,1,3072]{2,1,0:T(1,128)} %reshape.274), calls=%async_computation.1 | async-start | bytes 49152 | tf_op jit(solution)/shard_map/all_to_all | solution.py:148
  60.2 7.2 %all-to-all-start = ((bf16[32,64,256]{2,1,0:T(8,128)(2,1)}), bf16[32,64,256]{2,1,0:T(8,128)(2,1)S(1)}, u32[]{:S(2)}, u32[]{:S(2)}) async-start(bf16[32,64,256]{2,1,0:T(8,128)(2,1)} %pad_maximum_fusion), calls=%async_computation | async-start | bytes 2097152 | tf_op jit(solution)/shard_map/all_to_all | solution.py:38
  67.4 27.0 %all-to-all-start.2 = ((bf16[2,32,128,128]{3,2,0,1:T(8,128)(2,1)}), bf16[2,32,128,128]{3,2,0,1:T(8,128)(2,1)S(1)}, u32[]{:S(2)}, u32[]{:S(2)}) async-start(bf16[2,32,128,128]{3,2,0,1:T(8,128)(2,1)} %copy.260), calls=%async_computation.2 | async-start | bytes 4194304 | tf_op jit(solution)/shard_map/all_to_all | solution.py:147
  72.3 5.5 %copy-start.26 = (bf16[3,64,128]{2,1,0:T(8,128)(2,1)S(1)}, bf16[3,64,128]{2,1,0:T(8,128)(2,1)}, u32[]{:S(2)}) copy-start(bf16[3,64,128]{2,1,0:T(8,128)(2,1)} %param.32) | copy-start | bytes 147460
  72.3 6.1 %copy-start.20 = (bf16[3,4,128,64]{2,3,1,0:T(8,128)(2,1)S(1)}, bf16[3,4,128,64]{2,3,1,0:T(8,128)(2,1)}, u32[]{:S(2)}) copy-start(bf16[3,4,128,64]{2,3,1,0:T(8,128)(2,1)} %param.31) | copy-start | bytes 589828
  74.1 4.3 %copy-start.25 = (f32[16,128]{1,0:T(8,128)}, f32[16,128]{1,0:T(8,128)S(1)}, u32[]{:S(2)}) copy-start(f32[16,128]{1,0:T(8,128)S(1)} %broadcast_multiply_fusion.8) | copy-start | bytes 24580
  86.4 3.9 %copy-start.10 = (f32[16,128,128]{1,2,0:T(8,128)S(1)}, f32[16,128,128]{1,2,0:T(8,128)}, u32[]{:S(2)}) copy-start(f32[16,128,128]{1,2,0:T(8,128)} %copy-done.9) | copy-start | bytes 3145732
  86.4 3.9 %copy-start.28 = (f32[16,128]{1,0:T(8,128)S(1)}, f32[16,128]{1,0:T(8,128)}, u32[]{:S(2)}) copy-start(f32[16,128]{1,0:T(8,128)} %copy-done.27) | copy-start | bytes 24580
  86.4 3.9 %copy-start.30 = (f32[16,128]{1,0:T(8,128)S(1)}, f32[16,128]{1,0:T(8,128)}, u32[]{:S(2)}) copy-start(f32[16,128]{1,0:T(8,128)} %add_rsqrt_fusion.6) | copy-start | bytes 24580
  90.3 4.0 %copy-start.4 = (f32[6,16,128,128]{2,3,1,0:T(8,128)}, f32[6,16,128,128]{2,3,1,0:T(8,128)S(1)}, u32[]{:S(2)}) copy-start(f32[6,16,128,128]{2,3,1,0:T(8,128)S(1)} %add_bitcast_fusion.2) | copy-start | bytes 18874372
  100.4 6.1 %slice-start.2 = ((s8[6291456]{0:T(1024)(128)(4,1)}), s8[2097152]{0:T(1024)(128)(4,1)S(1)}, s32[]{:S(2)}) async-start(s8[6291456]{0:T(1024)(128)(4,1)} %bitcast.374), calls=%async_computation.6 | async-start | bytes 4194304
  103.3 3.9 %copy-start.11 = (f32[16,128,128]{1,2,0:T(8,128)S(1)}, f32[16,128,128]{1,2,0:T(8,128)}, u32[]{:S(2)}) copy-start(f32[16,128,128]{1,2,0:T(8,128)} %copy-done.9) | copy-start | bytes 3145732
  107.7 5.2 %copy-start.8 = (f32[16,128,128]{1,2,0:T(8,128)}, f32[16,128,128]{1,2,0:T(8,128)S(1)}, u32[]{:S(2)}) copy-start(f32[16,128,128]{1,2,0:T(8,128)S(1)} %get-tuple-element.26) | copy-start | bytes 3145732
  114.2 5.2 %copy-start.19 = (bf16[128,3,4,128]{3,0,2,1:T(8,128)(2,1)S(1)}, bf16[128,3,4,128]{3,0,2,1:T(8,128)(2,1)}, u32[]{:S(2)}) copy-start(bf16[128,3,4,128]{3,0,2,1:T(8,128)(2,1)} %copy.256) | copy-start | bytes 1179652
  123.4 4.9 %slice-start = ((s8[6291456]{0:T(1024)(128)(4,1)}), s8[2097152]{0:T(1024)(128)(4,1)S(1)}, s32[]{:S(2)}) async-start(s8[6291456]{0:T(1024)(128)(4,1)} %bitcast.372), calls=%async_computation.4 | async-start | bytes 4194304
  138.9 10.5 %copy-start.5 = (f32[6,16,128,128]{2,3,1,0:T(8,128)}, f32[6,16,128,128]{2,3,1,0:T(8,128)S(1)}, u32[]{:S(2)}) copy-start(f32[6,16,128,128]{2,3,1,0:T(8,128)S(1)} %add_bitcast_fusion) | copy-start | bytes 18874372
  139.1 4.3 %copy-start.3 = (f32[2,2,16,128,128]{3,4,2,0,1:T(8,128)S(1)}, f32[2,2,16,128,128]{3,4,2,0,1:T(8,128)}, u32[]{:S(2)}) copy-start(f32[2,2,16,128,128]{3,4,2,0,1:T(8,128)} %copy.261) | copy-start | bytes 12582916
  151.5 8.4 %copy-start.18 = (f32[3,32,64]{2,1,0:T(8,128)S(1)}, f32[3,32,64]{2,1,0:T(8,128)}, u32[]{:S(2)}) copy-start(f32[3,32,64]{2,1,0:T(8,128)} %copy-done.17) | copy-start | bytes 73732
  151.5 8.4 %copy-start.33 = (f32[3]{0:T(128)S(1)}, f32[3]{0:T(128)}, u32[]{:S(2)}) copy-start(f32[3]{0:T(128)} %copy-done.32) | copy-start | bytes 40
  151.5 9.1 %copy-start.1 = (bf16[512,384]{1,0:T(8,128)(2,1)S(1)}, bf16[512,384]{1,0:T(8,128)(2,1)}, u32[]{:S(2)}) copy-start(bf16[512,384]{1,0:T(8,128)(2,1)} %param.22) | copy-start | bytes 1179652
  (19 other events, 42.5 us)
where the time goes:
time: 162 us; the launch traced here: 161 us
  blocking collectives  50.7 us (31%)
  matrix products  43.7 us (27%)
  other arithmetic  27.4 us (17%)
  local copies, waits for them, and re-layouts  25.7 us (16%)
  starting transfers between devices  10.9 us (7%)
  between operations  2.19 us (1%)
    psum x4, blocking collectives, by_axis(): array = lax.psum(array, axis)  44.8 us
    unnamed x85, local copies, waits for them, and re-layouts  13.3 us
    sub x3, other arithmetic, window_net(): exponent = jnp.exp(scores - row_max)  10.9 us
    dot_general x3, matrix products, window_net(): jnp.einsum('wqh,hc->wqc', hidden, down_weight[block_index], preferred_ele...  10.8 us
    dot_general x3, matrix products, window_net(): jnp.einsum('wqc,jcd->jwqd', cond_norm, ada_weight[block_index], preferred...  8.58 us
    dot_general x3, matrix products, project_rows(): jnp.einsum('wqc,jcd->jwqd', portion, weight_set, preferred_element_type=j...  5.36 us
    dot_general x3, matrix products, window_net(): jnp.einsum('wqc,ch->wqh', normed_two, gateup_weight[block_index, 1], pref...  4.92 us
    dot_general x3, matrix products, window_net(): jnp.einsum('wqhd,wkhd->hwqk', query_rows, key_rows, preferred_element_typ...  4.54 us
  transfers between devices with their start and end apart: 3, of which 0 were waited for; matrix products, arithmetic and copies ran while one was open for 16% of the time, Pallas kernels for 0%

commit v1 on v0

--- a/solution.py
+++ b/solution.py
@@ -44,7 +44,7 @@
 
 def by_axis(array, axes):
     for axis in axes:
-        array = lax.psum(array, axis)
+        array = jnp.sum(lax.all_gather(array, axis), axis=0)
     return array
 
 

time: 162 us -> 171 us (1.056)
  local copies, waits for them, and re-layouts: 25.7 us -> 32.1 us
  between operations: 2.19 us -> 4.88 us
    psum x4 -> x0, blocking collectives: 44.8 us -> none  [by_axis(): array = lax.psum(array, axis)]
    unnamed x0 -> x4, blocking collectives: none -> 44.8 us
    unnamed x85 -> x97, local copies, waits for them, and re-layouts: 13.3 us -> 19.3 us
  transfers between devices with their start and end apart: 3 -> 3, of which waited for: 0 -> 0; matrix products, arithmetic and copies ran while one was open for 16% -> 15% of each run, Pallas kernels for 0% -> 0%
where the time goes in v1:
time: 171 us; the launch traced here: 170 us
  blocking collectives  50.7 us (30%)
  matrix products  43.7 us (26%)
  local copies, waits for them, and re-layouts  32.1 us (19%)
  other arithmetic  27.6 us (16%)
  starting transfers between devices  10.9 us (6%)
  between operations  4.88 us (3%)
    unnamed x4, blocking collectives  44.8 us
    unnamed x97, local copies, waits for them, and re-layouts  19.3 us
    sub x3, other arithmetic, window_net(): exponent = jnp.exp(scores - row_max)  10.9 us
    dot_general x3, matrix products, window_net(): jnp.einsum('wqh,hc->wqc', hidden, down_weight[block_index], preferred_ele...  10.8 us
    dot_general x3, matrix products, window_net(): jnp.einsum('wqc,jcd->jwqd', cond_norm, ada_weight[block_index], preferred...  8.58 us
    dot_general x3, matrix products, project_rows(): jnp.einsum('wqc,jcd->jwqd', portion, weight_set, preferred_element_type=j...  5.37 us
    dot_general x3, matrix products, window_net(): jnp.einsum('wqc,ch->wqh', normed_two, gateup_weight[block_index, 1], pref...  4.92 us
    dot_general x3, matrix products, window_net(): jnp.einsum('wqhd,wkhd->hwqk', query_rows, key_rows, preferred_element_typ...  4.55 us
  transfers between devices with their start and end apart: 3, of which 0 were waited for; matrix products, arithmetic and copies ran while one was open for 15% of the time, Pallas kernels for 0%

profile of v1, /device:TPU:1, one launch (start us, length us, event | category | flops | bytes accessed | tf_op | source)
XLA Modules:
  0.0 169.9 jit_solution(11048655311653837426)
XLA Ops:
  7.2 9.5 %all-reduce = f32[12]{0:T(128)S(1)} all-reduce(f32[12]{0:T(128)S(1)} %dynamic-update-slice), channel_id=2, replica_groups=mesh['win_0'=4,'win_1'=4,'win_2'=8,'head'=2] {'win_0'}, use_global_device_ids=true, to_apply=%add | all-reduce | flops 12 | bytes 96
  19.1 8.8 %all-reduce.1 = f32[12]{0:T(128)S(1)} all-reduce(f32[12]{0:T(128)S(1)} %dynamic-update-slice.1), channel_id=3, replica_groups=mesh['win_0'=4,'win_1'=4,'win_2'=8,'head'=2] {'win_1'}, use_global_device_ids=true, to_apply=%add.1 | all-reduce | flops 12 | bytes 96
  30.1 16.2 %all-reduce.2 = f32[24]{0:T(128)S(1)} all-reduce(f32[24]{0:T(128)S(1)} %dynamic-update-slice.2), channel_id=4, replica_groups=mesh['win_0'=4,'win_1'=4,'win_2'=8,'head'=2] {'win_2'}, use_global_device_ids=true, to_apply=%add.2 | all-reduce | flops 24 | bytes 192
  48.7 10.3 %all-reduce.3 = f32[6]{0:T(128)S(1)} all-reduce(f32[6]{0:T(128)S(1)} %dynamic-update-slice.3), channel_id=5, replica_groups=mesh['win_0'=4,'win_1'=4,'win_2'=8,'head'=2] {'head'}, use_global_device_ids=true, to_apply=%add.3 | all-reduce | flops 6 | bytes 48
  60.6 3.6 %all-to-all-start.1 = ((f32[2,1,3072]{2,1,0:T(1,128)}), f32[2,1,3072]{2,1,0:T(1,128)S(1)}, u32[]{:S(2)}, u32[]{:S(2)}) async-start(f32[2,1,3072]{2,1,0:T(1,128)} %reshape.300), calls=%async_computation.1 | async-start | bytes 49152 | tf_op jit(solution)/shard_map/all_to_all | solution.py:148
  66.6 2.2 %pad_maximum_fusion = bf16[32,64,256]{2,1,0:T(8,128)(2,1)} fusion(bf16[32,64,128]{2,1,0:T(8,128)(2,1)S(1)} %convolution_convert_fusion, bf16[32,64,128]{2,1,0:T(8,128)(2,1)} %param.21), kind=kLoop, calls=%fused_computation.139 | loop fusion | flops 2097152 | bytes 2097152 | tf_op jit(solution)/shard_map/concatenate | solution.py:35
  69.3 3.6 %all-to-all-start = ((bf16[32,64,256]{2,1,0:T(8,128)(2,1)}), bf16[32,64,256]{2,1,0:T(8,128)(2,1)S(1)}, u32[]{:S(2)}, u32[]{:S(2)}) async-start(bf16[32,64,256]{2,1,0:T(8,128)(2,1)} %pad_maximum_fusion), calls=%async_computation | async-start | bytes 2097152 | tf_op jit(solution)/shard_map/all_to_all | solution.py:38
  76.6 3.8 %all-to-all-start.2 = ((bf16[2,32,128,128]{3,2,0,1:T(8,128)(2,1)}), bf16[2,32,128,128]{3,2,0,1:T(8,128)(2,1)S(1)}, u32[]{:S(2)}, u32[]{:S(2)}) async-start(bf16[2,32,128,128]{3,2,0,1:T(8,128)(2,1)} %copy.260), calls=%async_computation.2 | async-start | bytes 4194304 | tf_op jit(solution)/shard_map/all_to_all | solution.py:147
  89.5 2.3 %all_gather.35 = bf16[128,1920]{1,0:T(8,128)(2,1)S(1)} all-gather(bf16[64,1920]{1,0:T(8,128)(2,1)S(1)} %pad_maximum_fusion.1), channel_id=1, replica_groups=mesh['win_0'=4,'win_1'=4,'win_2'=8,'head'=2] {'head'}, dimensions={0}, use_global_device_ids=true | all-gather | bytes 737280 | tf_op jit(solution)/shard_map/all_gather | solution.py:20
  97.6 2.0 %add_bitcast_fusion.2 = f32[6,16,128,128]{2,3,1,0:T(8,128)S(1)} fusion(f32[6,128]{1,0:T(8,128)S(1)} %get-tuple-element.19, bf16[16,128,128,1]{1,2,0,3:T(8,128)(2,1)S(1)} %fusion.118, bf16[3,6,128,128]{3,2,1,0:T(8,128)(2,1)} %param.29), kind=kOutput, calls=%fused_computation.5 | convolution fusion | flops 404226048 | bytes 7015424 | tf_op jit(solution)/shard_map/wqc,jcd->jwqd/dot_general | solution.py:84
  103.5 3.1 %copy.261 = f32[2,2,16,128,128]{3,4,2,0,1:T(8,128)} copy(bf16[2,2,16,128,128]{4,3,0,2,1:T(8,128)(2,1)S(1)} %bitcast.380) | data formatting | bytes 6291456 | tf_op jit(solution)/shard_map/convert_element_type | solution.py:106
  106.6 3.0 %bitcast_add_fusion.2 = f32[4,16,128,128]{2,3,1,0:T(8,128)S(1)} fusion(f32[2,2,16,128,128]{3,4,2,0,1:T(8,128)} %copy.261, bf16[16,128,4,32]{1,3,2,0:T(8,128)(2,1)S(1)} %bitcast.384, bf16[16,128,4,32]{1,3,2,0:T(8,128)(2,1)S(1)} %bitcast.383), kind=kOutput, calls=%fused_computation.8 | convolution fusion | flops 69206016 | bytes 9437184 | tf_op jit(solution)/shard_map/wqhd,wkhd->hwqk/dot_general | solution.py:103
  109.6 2.8 %fusion.188 = (f32[4,16,128]{2,1,0:T(8,128)S(1)}, f32[4,16,128,128]{2,3,1,0:T(8,128)}) fusion(f32[4,16,128,128]{2,3,1,0:T(8,128)S(1)} %bitcast_add_fusion.2), kind=kOutput, calls=%fused_computation.255 | output fusion | flops 2097279 | bytes 8421376 | tf_op jit(solution)/shard_map/sub | solution.py:108
  112.6 3.2 %fusion.39 = bf16[16,128,4,32]{1,3,2,0:T(8,128)(2,1)S(1)} fusion(f32[16,128,4,32]{1,3,2,0:T(8,128)S(1)} %bitcast.390, bf16[16,128,4,32]{1,3,2,0:T(8,128)(2,1)} %bitcast.396, f32[4,16,128,128]{2,3,1,0:T(8,128)} %get-tuple-element.24, f32[4,16,128]{2,1,0:T(8,128)S(1)} %get-tuple-element.23), kind=kOutput, calls=%fused_computation.49 | convolution fusion | flops 69730304 | bytes 6324224 | tf_op jit(solution)/shard_map/hwqk,wkhd->wqhd/dot_general | solution.py:110
  117.5 4.6 %add_bitcast_fusion.1 = f32[6,16,128,128]{2,3,1,0:T(8,128)} fusion(f32[6,128]{1,0:T(8,128)S(1)} %get-tuple-element.20, bf16[16,128,128,1]{1,2,0,3:T(8,128)(2,1)S(1)} %copy-done.7, bf16[3,6,128,128]{3,2,1,0:T(8,128)(2,1)} %param.29), kind=kOutput, calls=%fused_computation.4 | convolution fusion | flops 404226048 | bytes 7015424 | tf_op jit(solution)/shard_map/wqc,jcd->jwqd/dot_general | solution.py:84
  123.4 3.8 %fusion.190 = (f32[16,128]{1,0:T(8,128)S(1)}, f32[16,128,128]{1,2,0:T(8,128)}) fusion(f32[16,128,128]{1,2,0:T(8,128)} %copy-done.8, bf16[3,256,128]{2,1,0:T(8,128)(2,1)} %param.34, f32[16,128,256]{2,1,0:T(8,128)S(1)} %fusion.157, bf16[16,128,128]{1,2,0:T(8,128)(2,1)S(1)} %fusion.93, bf16[3,2,128,256]{3,2,1,0:T(8,128)(2,1)} %param.33, ...), kind=kOutput, calls=%fused_computation.257 | convolution fusion | flops 273152000 | bytes 5906432 | tf_op jit(solution)/shard_map/wqh,hc->wqc/dot_general | solution.py:136
  128.6 2.8 %convert_bitcast_fusion.1 = bf16[4,16,128,128]{2,3,1,0:T(8,128)(2,1)S(1)} fusion(f32[6,16,128,128]{2,3,1,0:T(8,128)} %add_bitcast_fusion.1, f32[16,128,128]{1,2,0:T(8,128)} %get-tuple-element.28, f32[16,128]{1,0:T(8,128)S(1)} %add_rsqrt_fusion.4, f32[16,128]{1,0:T(8,128)S(1)} %broadcast_multiply_fusion.5, bf16[3,4,128,128]{2,3,1,0:T(8,128)(2,1)S(1)} %bitcast.400), kind=kOutput, calls=%fused_computation.24 | convolution fusion | flops 271581184 | bytes 5390336 | tf_op jit(solution)/shard_map/wqc,jcd->jwqd/dot_general | solution.py:67
  132.6 4.1 %fusion.193 = (f32[4,16,128]{2,1,0:T(8,128)S(1)}, f32[4,16,128,128]{2,3,1,0:T(8,128)S(1)}) fusion(f32[4,16,128,128]{2,3,1,0:T(8,128)S(1)} %bitcast_add_fusion.1), kind=kOutput, calls=%fused_computation.258 | output fusion | flops 2097279 | bytes 8421376 | tf_op jit(solution)/shard_map/sub | solution.py:108
  142.1 4.0 %fusion.195 = (f32[16,128]{1,0:T(8,128)S(1)}, f32[16,128,128]{1,2,0:T(8,128)}) fusion(f32[16,128,128]{1,2,0:T(8,128)S(1)} %get-tuple-element.32, bf16[3,256,128]{2,1,0:T(8,128)(2,1)} %param.34, f32[16,128,256]{2,1,0:T(8,128)} %fusion.153, bf16[16,128,128]{1,2,0:T(8,128)(2,1)S(1)} %fusion.71, bf16[3,2,128,256]{3,2,1,0:T(8,128)(2,1)S(1)} %copy-done.24, ...), kind=kOutput, calls=%fused_computation.260 | convolution fusion | flops 273152000 | bytes 5906432 | tf_op jit(solution)/shard_map/wqh,hc->wqc/dot_general | solution.py:136
  146.1 2.0 %add_bitcast_fusion = f32[6,16,128,128]{2,3,1,0:T(8,128)S(1)} fusion(f32[6,128]{1,0:T(8,128)S(1)} %get-tuple-element.18, bf16[16,128,128,1]{1,2,0,3:T(8,128)(2,1)S(1)} %copy-done.7, bf16[3,6,128,128]{3,2,1,0:T(8,128)(2,1)} %param.29), kind=kOutput, calls=%fused_computation.3 | convolution fusion | flops 404226048 | bytes 7015424 | tf_op jit(solution)/shard_map/wqc,jcd->jwqd/dot_general | solution.py:84
  149.5 3.1 %copy-done.3 = f32[2,2,16,128,128]{3,4,2,0,1:T(8,128)S(1)} copy-done((f32[2,2,16,128,128]{3,4,2,0,1:T(8,128)S(1)}, f32[2,2,16,128,128]{3,4,2,0,1:T(8,128)}, u32[]{:S(2)}) %copy-start.3) | copy-done | bytes 4194328
  153.4 3.9 %fusion.198 = (f32[4,16,128]{2,1,0:T(8,128)S(1)}, f32[4,16,128,128]{2,3,1,0:T(8,128)S(1)}) fusion(f32[4,16,128,128]{2,3,1,0:T(8,128)S(1)} %bitcast_add_fusion), kind=kOutput, calls=%fused_computation.261 | output fusion | flops 2097279 | bytes 8421376 | tf_op jit(solution)/shard_map/sub | solution.py:108
  160.8 3.0 %fusion.200 = (f32[16,128]{1,0:T(8,128)S(1)}, f32[16,128,128]{1,2,0:T(8,128)S(1)}) fusion(f32[16,128,128]{1,2,0:T(8,128)S(1)} %get-tuple-element.38, bf16[3,256,128]{2,1,0:T(8,128)(2,1)} %param.34, f32[16,128,256]{2,1,0:T(8,128)} %fusion.149, bf16[16,128,128]{1,2,0:T(8,128)(2,1)S(1)} %fusion.49, bf16[3,2,128,256]{3,2,1,0:T(8,128)(2,1)S(1)} %copy-done.24, ...), kind=kOutput, calls=%fused_computation.263 | convolution fusion | flops 273152000 | bytes 5906432 | tf_op jit(solution)/shard_map/wqh,hc->wqc/dot_general | solution.py:136
  164.5 3.5 %all_to_all.54 = f32[2,1,3072]{2,1,0:T(1,128)S(1)} all-to-all(f32[2,1,3072]{2,1,0:T(1,128)S(1)} %reshape.302), channel_id=1, replica_groups=mesh['win_0'=4,'win_1'=4,'win_2'=8,'head'=2] {'head'}, dimensions={0} | all-to-all | bytes 49152 | tf_op jit(solution)/shard_map/all_to_all | solution.py:161
  (191 shorter events, 55.8 us)
Async XLA Ops:
  0.0 64.2 %copy-start = (bf16[512,384]{1,0:T(8,128)(2,1)S(1)}, bf16[512,384]{1,0:T(8,128)(2,1)}, u32[]{:S(2)}) copy-start(bf16[512,384]{1,0:T(8,128)(2,1)} %param.22) | copy-start | bytes 1179652
  0.0 75.1 %copy-start.12 = (bf16[2,32,128,128]{3,2,1,0:T(8,128)(2,1)S(1)}, bf16[2,32,128,128]{3,2,1,0:T(8,128)(2,1)}, u32[]{:S(2)}) copy-start(bf16[2,32,128,128]{3,2,1,0:T(8,128)(2,1)} %param.25) | copy-start | bytes 6291460
  5.6 63.1 %copy-start.17 = (f32[3,32,64]{2,1,0:T(8,128)}, f32[3,32,64]{2,1,0:T(8,128)S(1)}, u32[]{:S(2)}) copy-start(f32[3,32,64]{2,1,0:T(8,128)S(1)} %get-tuple-element.6) | copy-start | bytes 73732
  59.8 16.8 %copy-start.32 = (f32[3]{0:T(128)}, f32[3]{0:T(128)S(1)}, u32[]{:S(2)}) copy-start(f32[3]{0:T(128)S(1)} %broadcast_divide_fusion) | copy-start | bytes 40
  60.6 8.1 %all-to-all-start.1 = ((f32[2,1,3072]{2,1,0:T(1,128)}), f32[2,1,3072]{2,1,0:T(1,128)S(1)}, u32[]{:S(2)}, u32[]{:S(2)}) async-start(f32[2,1,3072]{2,1,0:T(1,128)} %reshape.300), calls=%async_computation.1 | async-start | bytes 49152 | tf_op jit(solution)/shard_map/all_to_all | solution.py:148
  69.3 7.2 %all-to-all-start = ((bf16[32,64,256]{2,1,0:T(8,128)(2,1)}), bf16[32,64,256]{2,1,0:T(8,128)(2,1)S(1)}, u32[]{:S(2)}, u32[]{:S(2)}) async-start(bf16[32,64,256]{2,1,0:T(8,128)(2,1)} %pad_maximum_fusion), calls=%async_computation | async-start | bytes 2097152 | tf_op jit(solution)/shard_map/all_to_all | solution.py:38
  76.6 27.0 %all-to-all-start.2 = ((bf16[2,32,128,128]{3,2,0,1:T(8,128)(2,1)}), bf16[2,32,128,128]{3,2,0,1:T(8,128)(2,1)S(1)}, u32[]{:S(2)}, u32[]{:S(2)}) async-start(bf16[2,32,128,128]{3,2,0,1:T(8,128)(2,1)} %copy.260), calls=%async_computation.2 | async-start | bytes 4194304 | tf_op jit(solution)/shard_map/all_to_all | solution.py:147
  81.5 5.5 %copy-start.26 = (bf16[3,64,128]{2,1,0:T(8,128)(2,1)S(1)}, bf16[3,64,128]{2,1,0:T(8,128)(2,1)}, u32[]{:S(2)}) copy-start(bf16[3,64,128]{2,1,0:T(8,128)(2,1)} %param.32) | copy-start | bytes 147460
  81.5 6.1 %copy-start.20 = (bf16[3,4,128,64]{2,3,1,0:T(8,128)(2,1)S(1)}, bf16[3,4,128,64]{2,3,1,0:T(8,128)(2,1)}, u32[]{:S(2)}) copy-start(bf16[3,4,128,64]{2,3,1,0:T(8,128)(2,1)} %param.31) | copy-start | bytes 589828
  83.3 4.3 %copy-start.25 = (f32[16,128]{1,0:T(8,128)}, f32[16,128]{1,0:T(8,128)S(1)}, u32[]{:S(2)}) copy-start(f32[16,128]{1,0:T(8,128)S(1)} %broadcast_multiply_fusion.8) | copy-start | bytes 24580
  95.6 3.9 %copy-start.10 = (f32[16,128,128]{1,2,0:T(8,128)S(1)}, f32[16,128,128]{1,2,0:T(8,128)}, u32[]{:S(2)}) copy-start(f32[16,128,128]{1,2,0:T(8,128)} %copy-done.9) | copy-start | bytes 3145732
  95.6 3.9 %copy-start.28 = (f32[16,128]{1,0:T(8,128)S(1)}, f32[16,128]{1,0:T(8,128)}, u32[]{:S(2)}) copy-start(f32[16,128]{1,0:T(8,128)} %copy-done.27) | copy-start | bytes 24580
  95.6 3.9 %copy-start.30 = (f32[16,128]{1,0:T(8,128)S(1)}, f32[16,128]{1,0:T(8,128)}, u32[]{:S(2)}) copy-start(f32[16,128]{1,0:T(8,128)} %add_rsqrt_fusion.6) | copy-start | bytes 24580
  99.5 4.0 %copy-start.4 = (f32[6,16,128,128]{2,3,1,0:T(8,128)}, f32[6,16,128,128]{2,3,1,0:T(8,128)S(1)}, u32[]{:S(2)}) copy-start(f32[6,16,128,128]{2,3,1,0:T(8,128)S(1)} %add_bitcast_fusion.2) | copy-start | bytes 18874372
  109.6 6.1 %slice-start.2 = ((s8[6291456]{0:T(1024)(128)(4,1)}), s8[2097152]{0:T(1024)(128)(4,1)S(1)}, s32[]{:S(2)}) async-start(s8[6291456]{0:T(1024)(128)(4,1)} %bitcast.378), calls=%async_computation.6 | async-start | bytes 4194304
  112.6 3.9 %copy-start.11 = (f32[16,128,128]{1,2,0:T(8,128)S(1)}, f32[16,128,128]{1,2,0:T(8,128)}, u32[]{:S(2)}) copy-start(f32[16,128,128]{1,2,0:T(8,128)} %copy-done.9) | copy-start | bytes 3145732
  116.9 5.2 %copy-start.8 = (f32[16,128,128]{1,2,0:T(8,128)}, f32[16,128,128]{1,2,0:T(8,128)S(1)}, u32[]{:S(2)}) copy-start(f32[16,128,128]{1,2,0:T(8,128)S(1)} %get-tuple-element.26) | copy-start | bytes 3145732
  123.4 5.2 %copy-start.19 = (bf16[128,3,4,128]{3,0,2,1:T(8,128)(2,1)S(1)}, bf16[128,3,4,128]{3,0,2,1:T(8,128)(2,1)}, u32[]{:S(2)}) copy-start(bf16[128,3,4,128]{3,0,2,1:T(8,128)(2,1)} %copy.256) | copy-start | bytes 1179652
  132.6 4.9 %slice-start = ((s8[6291456]{0:T(1024)(128)(4,1)}), s8[2097152]{0:T(1024)(128)(4,1)S(1)}, s32[]{:S(2)}) async-start(s8[6291456]{0:T(1024)(128)(4,1)} %bitcast.376), calls=%async_computation.4 | async-start | bytes 4194304
  148.1 10.5 %copy-start.5 = (f32[6,16,128,128]{2,3,1,0:T(8,128)}, f32[6,16,128,128]{2,3,1,0:T(8,128)S(1)}, u32[]{:S(2)}) copy-start(f32[6,16,128,128]{2,3,1,0:T(8,128)S(1)} %add_bitcast_fusion) | copy-start | bytes 18874372
  148.3 4.3 %copy-start.3 = (f32[2,2,16,128,128]{3,4,2,0,1:T(8,128)S(1)}, f32[2,2,16,128,128]{3,4,2,0,1:T(8,128)}, u32[]{:S(2)}) copy-start(f32[2,2,16,128,128]{3,4,2,0,1:T(8,128)} %copy.261) | copy-start | bytes 12582916
  160.7 8.4 %copy-start.18 = (f32[3,32,64]{2,1,0:T(8,128)S(1)}, f32[3,32,64]{2,1,0:T(8,128)}, u32[]{:S(2)}) copy-start(f32[3,32,64]{2,1,0:T(8,128)} %copy-done.17) | copy-start | bytes 73732
  160.7 8.4 %copy-start.33 = (f32[3]{0:T(128)S(1)}, f32[3]{0:T(128)}, u32[]{:S(2)}) copy-start(f32[3]{0:T(128)} %copy-done.32) | copy-start | bytes 40
  160.7 9.1 %copy-start.1 = (bf16[512,384]{1,0:T(8,128)(2,1)S(1)}, bf16[512,384]{1,0:T(8,128)(2,1)}, u32[]{:S(2)}) copy-start(bf16[512,384]{1,0:T(8,128)(2,1)} %param.22) | copy-start | bytes 1179652
  (19 other events, 42.5 us)
